TPU v7x, 32 devices: a whole 2x2x4 slice. The times are simulated.
32 devices in a mesh: gz: 16 (over z, y, x), gy: 2 (over core).
Axes of the slice: x: 2, y: 2, z: 4, core: 2. Of those that a mesh axis runs over, the one named last changes fastest.
Arguments:
- snapshots: float32 [48, 64, 128, 256], P(None, 'gz', 'gy'), may hold values from -6 to 6
- energies: float32 [48], replicated, may hold values from 0.3 to 3
- plane_weight: float32 [64], P('gz'), may hold values from 1 to 10
Outputs:
- modes: float32 [16, 64, 128, 256], P(None, 'gz', 'gy')
- basis: float32 [48, 16], replicated
All inputs are finite; a program needn't handle non-finite values.
Results may differ from a plain program's by a relative error of at most 0.0003.
Values sent between devices are 32-bit elements; how exact they have to be, the bound alone decides.
A program may use at most 128 MiB of HBM per device.

v0:
```python
import jax
import jax.numpy as jnp
from jax import lax
from jax.sharding import PartitionSpec as P

MODES = 16
ITERS = 6


def padded_2(block, sides, width):
    for axis, dim in sides:
        count = lax.axis_size(axis)
        forward = [(i, i + 1) for i in range(count - 1)]
        forward.append((count - 1, 0))
        backward = [(target, source) for source, target in forward]
        low = lax.ppermute(
            lax.slice_in_dim(block, block.shape[dim] - width, None, axis=dim), axis, forward
        )
        high = lax.ppermute(lax.slice_in_dim(block, 0, width, axis=dim), axis, backward)
        block = jnp.concatenate([low, block, high], axis=dim)
    return block


def local(snapshots, energies, plane_weight):
    count, planes, rows, width = snapshots.shape
    total = planes * lax.axis_size("gz") * rows * lax.axis_size("gy") * width
    scaled = snapshots * energies[:, None, None, None]
    padded = padded_2(scaled, (("gz", 1),), 1)
    filtered = 0.25 * padded[:, :-2] + 0.5 * scaled + 0.25 * padded[:, 2:]
    flat = filtered.reshape(count, -1)
    weighted = (filtered * plane_weight[None, :, None, None]).reshape(count, -1)
    partial_value = jnp.dot(weighted, flat.T, precision=lax.Precision.HIGHEST) / total
    gram = lax.psum(partial_value, ("gz", "gy"))
    basis = jnp.eye(count, dtype=jnp.float32)[:, :MODES]
    for step in range(ITERS):
        image = jnp.dot(gram, basis, precision=lax.Precision.HIGHEST)
        factor = jnp.linalg.cholesky(jnp.dot(image.T, image, precision=lax.Precision.HIGHEST))
        basis = jax.scipy.linalg.solve_triangular(factor, image.T, lower=True).T
    raw = jnp.dot(basis.T, flat, precision=lax.Precision.HIGHEST).reshape(
        MODES, planes, rows, width
    )
    projected = jnp.dot(gram, basis, precision=lax.Precision.HIGHEST)
    norms = jnp.sum(basis * projected, axis=0)
    modes = raw / jnp.sqrt(norms)[:, None, None, None]
    return (modes, basis)


def solution(mesh):
    placed = (P(None, "gz", "gy", None), P(), P("gz"))
    return jax.shard_map(
        local,
        mesh=mesh,
        in_specs=placed,
        out_specs=(P(None, "gz", "gy", None), P()),
        check_vma=False,
    )
```

profile of v0, /device:TPU:0, one launch (start us, length us, event | category | flops | bytes accessed | tf_op | source)
XLA Modules:
  0.0 292.3 jit_solution(18266743144551200550)
XLA Ops:
  0.6 12.0 %broadcast_multiply_fusion.1 = f32[48,4,64,256]{3,2,1,0:T(8,128)} fusion(f32[48,4,64,256]{3,2,1,0:T(8,128)} %param.6, f32[48]{0:T(128)} %param.7), kind=kLoop, calls=%fused_computation.12 | loop fusion | flops 3145728 | bytes 25166016 | tf_op jit(solution)/shard_map/mul | solution.py:27
  12.7 3.7 %fusion.67 = (f32[48,1,64,256]{3,2,1,0:T(8,128)S(1)}, f32[48,1,64,256]{3,2,1,0:T(8,128)S(1)}) fusion(f32[48,4,64,256]{3,2,1,0:T(8,128)} %broadcast_multiply_fusion.1), kind=kLoop, calls=%fused_computation.84 | loop fusion | bytes 12582912 | tf_op jit(solution)/shard_map/slice | solution.py:17
  16.4 3.0 %collective-permute-start = (f32[48,1,64,256]{3,2,1,0:T(8,128)S(1)}, f32[48,1,64,256]{3,2,1,0:T(8,128)}, u32[]{:S(2)}, u32[]{:S(2)}) collective-permute-start(f32[48,1,64,256]{3,2,1,0:T(8,128)S(1)} %get-tuple-element.10), channel_id=1, source_target_pairs={{0,2},{2,4},{4,6},{6,8},{8,10},{10,12},{12,14},{14,16},{16,18},{18... | collective-permute-start | bytes 9437192 | tf_op jit(solution)/shard_map/ppermute | solution.py:16
  19.4 4.1 %collective-permute-start.1 = (f32[48,1,64,256]{3,2,1,0:T(8,128)S(1)}, f32[48,1,64,256]{3,2,1,0:T(8,128)}, u32[]{:S(2)}, u32[]{:S(2)}) collective-permute-start(f32[48,1,64,256]{3,2,1,0:T(8,128)S(1)} %get-tuple-element.11), channel_id=1, source_target_pairs={{2,0},{4,2},{6,4},{8,6},{10,8},{12,10},{14,12},{16,14},{18,16},{20... | collective-permute-start | bytes 9437192 | tf_op jit(solution)/shard_map/ppermute | solution.py:19
  23.5 130.7 %collective-permute-done = f32[48,1,64,256]{3,2,1,0:T(8,128)} collective-permute-done((f32[48,1,64,256]{3,2,1,0:T(8,128)S(1)}, f32[48,1,64,256]{3,2,1,0:T(8,128)}, u32[]{:S(2)}, u32[]{:S(2)}) %collective-permute-start) | collective-permute-done | bytes 3145760 | tf_op jit(solution)/shard_map/ppermute | solution.py:16
  154.2 2.1 collective-permute-done.1
  156.3 13.5 %broadcast_multiply_fusion = (f32[48,4,64,256]{3,2,1,0:T(8,128)}, f32[48,4,64,256]{3,2,1,0:T(8,128)}) fusion(f32[4]{0:T(128)S(1)} %copy-done.2, f32[48,1,64,256]{3,2,1,0:T(8,128)} %collective-permute-done.1, f32[48,4,64,256]{3,2,1,0:T(8,128)S(1)} %copy-done, f32[48,1,64,256]{3,2,1,0:T(8,128)} %collective-permute-done), kind=kLoop, calls=%fused_computation.11 | loop fusion | flops 25165824 | bytes 44040208 | tf_op jit(solution)/shard_map/mul | solution.py:31
  169.7 32.1 %fusion.16 = f32[48,48]{1,0:T(8,128)S(1)} fusion(f32[48,4,64,256]{3,2,1,0:T(8,128)} %get-tuple-element.9, f32[48,4,64,256]{3,2,1,0:T(8,128)} %get-tuple-element.8), kind=kOutput, calls=%fused_computation.15 | convolution fusion | flops 1811941632 | bytes 25175040 | tf_op jit(solution)/shard_map/dot_general | solution.py:32
  201.8 39.7 %psum.7 = f32[48,48]{1,0:T(8,128)S(1)} all-reduce(f32[48,48]{1,0:T(8,128)S(1)} %fusion.16), channel_id=1, replica_groups=mesh['gz'=16,'gy'=2] {'gz','gy'}, use_global_device_ids=true, to_apply=%region_0.0 | all-reduce | flops 2304 | bytes 18432 | tf_op jit(solution)/shard_map/psum | solution.py:33
  242.0 1.5 cholesky.104
  243.5 0.6 compare_reduce_fusion.5
  244.1 0.6 fusion.24
  244.8 1.2 custom-call.10
  246.6 1.5 cholesky.115
  248.8 0.6 fusion.25
  249.4 1.2 custom-call.11
  251.2 1.5 cholesky.126
  252.7 0.6 compare_reduce_fusion.3
  253.4 0.6 fusion.26
  254.0 1.2 custom-call.12
  255.8 1.5 cholesky.137
  258.0 0.6 fusion.27
  258.7 1.2 custom-call.13
  260.5 1.5 cholesky.148
  262.0 0.6 compare_reduce_fusion.1
  262.6 0.6 fusion.28
  263.3 1.2 custom-call.14
  265.1 1.5 cholesky.159
  267.2 0.6 fusion.29
  267.9 1.2 custom-call.15
  269.6 18.2 %broadcast_divide_fusion = f32[16,4,64,256]{3,0,2,1:T(8,128)S(1)} fusion(f32[16]{0:T(128)S(1)} %sqrt.7, f32[4,64,256,48]{2,1,0,3:T(8,128)} %bitcast.120, f32[16,48]{1,0:T(8,128)S(1)} %fusion.31), kind=kOutput, calls=%fused_computation.13 | convolution fusion | flops 605028352 | bytes 16780352 | tf_op jit(solution)/shard_map/dot_general | solution.py:39
  287.8 4.4 %copy.23 = f32[16,4,64,256]{3,2,1,0:T(8,128)} copy(f32[16,4,64,256]{3,0,2,1:T(8,128)S(1)} %broadcast_divide_fusion) | data formatting | bytes 8388608
  (47 shorter events, 6.0 us)
Async XLA Ops:
  12.7 143.6 %copy-start = (f32[48,4,64,256]{3,2,1,0:T(8,128)S(1)}, f32[48,4,64,256]{3,2,1,0:T(8,128)}, u32[]{:S(2)}) copy-start(f32[48,4,64,256]{3,2,1,0:T(8,128)} %broadcast_multiply_fusion.1) | copy-start | bytes 37748740
  12.7 143.6 %copy-start.2 = (f32[4]{0:T(128)S(1)}, f32[4]{0:T(128)}, u32[]{:S(2)}) copy-start(f32[4]{0:T(128)} %param.8) | copy-start | bytes 52
  16.4 137.8 %collective-permute-start = (f32[48,1,64,256]{3,2,1,0:T(8,128)S(1)}, f32[48,1,64,256]{3,2,1,0:T(8,128)}, u32[]{:S(2)}, u32[]{:S(2)}) collective-permute-start(f32[48,1,64,256]{3,2,1,0:T(8,128)S(1)} %get-tuple-element.10), channel_id=1, source_target_pairs={{0,2},{2,4},{4,6},{6,8},{8,10},{10,12},{12,14},{14,16},{16,18},{18... | collective-permute-start | bytes 9437192 | tf_op jit(solution)/shard_map/ppermute | solution.py:16
  19.4 136.8 %collective-permute-start.1 = (f32[48,1,64,256]{3,2,1,0:T(8,128)S(1)}, f32[48,1,64,256]{3,2,1,0:T(8,128)}, u32[]{:S(2)}, u32[]{:S(2)}) collective-permute-start(f32[48,1,64,256]{3,2,1,0:T(8,128)S(1)} %get-tuple-element.11), channel_id=1, source_target_pairs={{2,0},{4,2},{6,4},{8,6},{10,8},{12,10},{14,12},{16,14},{18,16},{20... | collective-permute-start | bytes 9437192 | tf_op jit(solution)/shard_map/ppermute | solution.py:19
  269.3 22.9 %copy-start.1 = (f32[16,48]{1,0:T(8,128)}, f32[16,48]{1,0:T(8,128)S(1)}, u32[]{:S(2)}) copy-start(f32[16,48]{1,0:T(8,128)S(1)} %fusion.31) | copy-start | bytes 9220
where the time goes:
time: 293 us; the launch traced here: 292 us
  waiting for transfers between devices  133 us (45%)
  matrix products  53.6 us (18%)
  other arithmetic  49.7 us (17%)
  blocking collectives  39.7 us (14%)
  local copies, waits for them, and re-layouts  8.63 us (3%)
  starting transfers between devices  7.08 us (2%)
    ppermute x1, waiting for transfers between devices, padded_2(): lax.ppermute(lax.slice_in_dim(block, block.shape[dim] - width, None, axis...  131 us
    psum x1, blocking collectives, local(): gram = lax.psum(partial_value, ('gz', 'gy'))  39.7 us
    dot_general x1, matrix products, local(): jnp.dot(weighted, flat.T, precision=lax.Precision.HIGHEST) / total  32.1 us
    dot_general x1, matrix products, local(): jnp.dot(basis.T, flat, precision=lax.Precision.HIGHEST)  18.2 us
    mul x1, other arithmetic, local(): weighted = (filtered * plane_weight[None, :, None, None]).reshape(count, -1)  13.5 us
    another operation x18, other arithmetic, local(): jnp.linalg.cholesky(jnp.dot(image.T, image, precision=lax.Precision.HIGHE...  12.9 us
    mul x1, other arithmetic, local(): scaled = snapshots * energies[:, None, None, None]  12 us
    another operation x12, other arithmetic, local(): basis = jax.scipy.linalg.solve_triangular(factor, image.T, lower=True).T  11.3 us
  transfers between devices with their start and end apart: 2, of which 2 were waited for; matrix products, arithmetic and copies ran while one was open for 0% of the time, Pallas kernels for 0%

commit v1 on v0

v1 whole, which is shorter than its diff:
```python
import functools

import jax
import jax.numpy as jnp
from jax import lax
from jax.experimental import pallas as pl
from jax.experimental.pallas import tpu as pltpu
from jax.sharding import PartitionSpec as P

MODES = 16
ITERS = 6
CHUNK = 8
LANES = 128
MESH = pl.DeviceIdType.MESH
HIGHEST = lax.Precision.HIGHEST
NT = (((1,), (1,)), ((), ()))


def butterfly(index, bit):
    return index + bit - 2 * bit * lax.rem(lax.div(index, bit), 2)


def bits_of(count):
    return [1 << k for k in range(count.bit_length() - 1)]


def gram_kernel(
    gz_count, gy_count, total,
    snap_ref, energy_ref, weight_ref, split_ref, gram_ref,
    own, halo, split, sums, arrived, own_sem, halo_send, halo_recv, split_sem, sum_send, sum_recv,
):
    count, planes, rows, width = snap_ref.shape
    chunks = rows // CHUNK
    halves = width // LANES
    me = lax.axis_index("gz")
    core = lax.axis_index("gy")
    right = lax.rem(me + 1, gz_count)
    left = lax.rem(me + gz_count - 1, gz_count)

    loads = [
        pltpu.make_async_copy(
            snap_ref.at[:, z, :, pl.ds(h * LANES, LANES)], own.at[z, h], own_sem.at[z, h]
        )
        for z in range(planes)
        for h in range(halves)
    ]
    for load in loads:
        load.start()

    partners = [{"gy": butterfly(core, bit)} for bit in bits_of(gy_count)]
    partners += [{"gz": butterfly(me, bit)} for bit in bits_of(gz_count)]
    barrier = pltpu.get_barrier_semaphore()
    greeted = [{"gz": left}, {"gz": right}] + partners
    for device in greeted:
        pl.semaphore_signal(barrier, inc=1, device_id=device, device_id_type=MESH)
    pl.semaphore_wait(barrier, len(greeted))

    def halo_copy(side, chunk, h):
        span = pl.ds(pl.multiple_of(chunk * CHUNK, CHUNK), CHUNK)
        return pltpu.make_async_remote_copy(
            src_ref=snap_ref.at[
                :, planes - 1 if side == 0 else 0, span, pl.ds(h * LANES, LANES)
            ],
            dst_ref=halo.at[side, h, :, span],
            send_sem=halo_send.at[side, h, chunk],
            recv_sem=halo_recv.at[side, h, chunk],
            device_id={"gz": right if side == 0 else left},
            device_id_type=MESH,
        )

    def send(chunk, carry):
        for h in range(halves):
            halo_copy(0, chunk, h).start()
            halo_copy(1, chunk, h).start()
        return carry

    lax.fori_loop(0, chunks, send, 0)
    for load in loads:
        load.wait()

    energy = jnp.broadcast_to(energy_ref[...], (count, LANES))

    def flat(ref):
        return [ref.at[h].reshape(count * rows, LANES) for h in range(halves)]

    stack = [flat(halo.at[0])] + [flat(own.at[z]) for z in range(planes)] + [flat(halo.at[1])]

    def split_copy(z, chunk):
        span = pl.ds(chunk * CHUNK, CHUNK)
        return pltpu.make_async_copy(
            split.at[z, span], split_ref.at[z, span], split_sem.at[z, chunk]
        )

    def add_rows(z, chunk, acc):
        below, middle, above = stack[z : z + 3]
        for r in range(CHUNK):
            y = chunk * CHUNK + r
            line = pl.ds(y, count, stride=rows)
            pieces = [
                energy * (0.25 * (b[line, :] + a[line, :]) + 0.5 * m[line, :])
                for b, m, a in zip(below, middle, above)
            ]
            value = jnp.concatenate(pieces, axis=1)
            high = value.astype(jnp.bfloat16)
            low = (value - high.astype(jnp.float32)).astype(jnp.bfloat16)
            both = jnp.concatenate([high, low], axis=0)
            split[z, y] = both
            first = lax.dot_general(both, high, NT, preferred_element_type=jnp.float32)
            second = lax.dot_general(high, low, NT, preferred_element_type=jnp.float32)
            acc = acc + (first[:count] + (first[count:] + second))
        split_copy(z, chunk).start()
        return acc

    zero = jnp.zeros((count, count), jnp.float32)
    gram = zero
    for z in range(1, planes - 1):
        acc = lax.fori_loop(0, chunks, functools.partial(add_rows, z), zero)
        gram = gram + weight_ref[z] * acc

    def edge(chunk, carry):
        for h in range(halves):
            halo_copy(0, chunk, h).wait_recv()
        first = add_rows(0, chunk, carry[0])
        for h in range(halves):
            halo_copy(1, chunk, h).wait_recv()
        return first, add_rows(planes - 1, chunk, carry[1])

    first, last = lax.fori_loop(0, chunks, edge, (zero, zero))
    gram = (gram + weight_ref[0] * first + weight_ref[planes - 1] * last) / total

    for step, partner in enumerate(partners):
        sums[step] = gram
        copy = pltpu.make_async_remote_copy(
            src_ref=sums.at[step],
            dst_ref=arrived.at[step],
            send_sem=sum_send.at[step],
            recv_sem=sum_recv.at[step],
            device_id=partner,
            device_id_type=MESH,
        )
        copy.start()
        copy.wait()
        gram = gram + arrived[step]
    gram_ref[...] = gram

    def drain(chunk, carry):
        for h in range(halves):
            halo_copy(0, chunk, h).wait_send()
            halo_copy(1, chunk, h).wait_send()
        for z in range(planes):
            split_copy(z, chunk).wait()
        return carry

    lax.fori_loop(0, chunks, drain, 0)


def modes_kernel(gram_ref, split_ref, modes_ref, basis_ref, split, staged, in_sem, out_sem):
    planes, rows, _, width = split_ref.shape
    count = gram_ref.shape[0]
    parts = in_sem.shape[1]
    part = rows // parts
    halves = width // LANES

    def load(z, p):
        span = pl.ds(p * part, part)
        return pltpu.make_async_copy(split_ref.at[z, span], split.at[z, span], in_sem.at[z, p])

    def store(z, p, h):
        span = pl.ds(pl.multiple_of(p * part, part), part)
        return pltpu.make_async_copy(
            staged.at[z, h, :, span],
            modes_ref.at[:, z, span, pl.ds(h * LANES, LANES)],
            out_sem.at[z, h, p],
        )

    for z in range(planes):
        for p in range(parts):
            load(z, p).start()

    gram = gram_ref[...]
    row = lax.broadcasted_iota(jnp.int32, (MODES, 1), 0)
    diagonal = (
        lax.broadcasted_iota(jnp.int32, (MODES, MODES), 0)
        == lax.broadcasted_iota(jnp.int32, (MODES, MODES), 1)
    )

    def iterate(step, basis):
        image = jnp.dot(basis, gram, precision=HIGHEST, preferred_element_type=jnp.float32)
        square = lax.dot_general(
            image, image, NT, precision=HIGHEST, preferred_element_type=jnp.float32
        )
        for j in range(MODES - 1):
            inverse = 1.0 / square[j : j + 1, j : j + 1]
            ratio = jnp.where(row > j, square[:, j : j + 1] * inverse, 0.0)
            image = image - ratio * image[j : j + 1, :]
            square = square - ratio * square[j : j + 1, :]
        pivots = jnp.sum(jnp.where(diagonal, square, 0.0), axis=1, keepdims=True)
        return image / jnp.sqrt(pivots)

    start = (
        lax.broadcasted_iota(jnp.int32, (MODES, count), 0)
        == lax.broadcasted_iota(jnp.int32, (MODES, count), 1)
    ).astype(jnp.float32)
    basis = lax.fori_loop(0, ITERS, iterate, start)
    basis_ref[...] = basis.T
    projected = jnp.dot(basis, gram, precision=HIGHEST, preferred_element_type=jnp.float32)
    norms = jnp.sum(basis * projected, axis=1, keepdims=True)
    scaled = basis / jnp.sqrt(norms)
    high = scaled.astype(jnp.bfloat16)
    low = (scaled - high.astype(jnp.float32)).astype(jnp.bfloat16)
    both = jnp.concatenate([high, low], axis=0)

    for z in range(planes):
        flat = [staged.at[z, h].reshape(MODES * rows, LANES) for h in range(halves)]

        def do_part(p, carry):
            load(z, p).wait()

            def group(g, carry):
                for r in range(8):
                    y = p * part + g * 8 + r
                    first = jnp.dot(
                        both, split[z, y, :count], preferred_element_type=jnp.float32
                    )
                    second = jnp.dot(
                        high, split[z, y, count:], preferred_element_type=jnp.float32
                    )
                    raw = first[:MODES] + (first[MODES:] + second)
                    for h in range(halves):
                        flat[h][pl.ds(y, MODES, stride=rows), :] = raw[
                            :, h * LANES : (h + 1) * LANES
                        ]
                return carry

            lax.fori_loop(0, part // 8, group, 0)
            for h in range(halves):
                store(z, p, h).start()
            return carry

        lax.fori_loop(0, parts, do_part, 0)
    for z in range(planes):
        for p in range(parts):
            for h in range(halves):
                store(z, p, h).wait()


def local(gz_count, gy_count, snapshots, energies, plane_weight):
    count, planes, rows, width = snapshots.shape
    total = planes * gz_count * rows * gy_count * width
    chunks = rows // CHUNK
    halves = width // LANES
    steps = len(bits_of(gz_count)) + len(bits_of(gy_count))
    anywhere = pl.BlockSpec(memory_space=pl.ANY)
    vmem = pl.BlockSpec(memory_space=pltpu.VMEM)
    split, gram = pl.pallas_call(
        functools.partial(gram_kernel, gz_count, gy_count, total),
        name="exchange_and_gram",
        out_shape=(
            jax.ShapeDtypeStruct((planes, rows, 2 * count, width), jnp.bfloat16),
            jax.ShapeDtypeStruct((count, count), jnp.float32),
        ),
        in_specs=[anywhere, vmem, pl.BlockSpec(memory_space=pltpu.SMEM)],
        out_specs=(anywhere, vmem),
        scratch_shapes=[
            pltpu.VMEM((planes, halves, count, rows, LANES), jnp.float32),
            pltpu.VMEM((2, halves, count, rows, LANES), jnp.float32),
            pltpu.VMEM((planes, rows, 2 * count, width), jnp.bfloat16),
            pltpu.VMEM((steps, count, count), jnp.float32),
            pltpu.VMEM((steps, count, count), jnp.float32),
            pltpu.SemaphoreType.DMA((planes, halves)),
            pltpu.SemaphoreType.DMA((2, halves, chunks)),
            pltpu.SemaphoreType.DMA((2, halves, chunks)),
            pltpu.SemaphoreType.DMA((planes, chunks)),
            pltpu.SemaphoreType.DMA((steps,)),
            pltpu.SemaphoreType.DMA((steps,)),
        ],
        compiler_params=pltpu.CompilerParams(
            collective_id=0, has_side_effects=True, vmem_limit_bytes=60 * 1024 * 1024
        ),
    )(snapshots, energies[:, None], plane_weight)
    parts = 4
    modes, basis = pl.pallas_call(
        modes_kernel,
        name="basis_and_modes",
        out_shape=(
            jax.ShapeDtypeStruct((MODES, planes, rows, width), jnp.float32),
            jax.ShapeDtypeStruct((count, MODES), jnp.float32),
        ),
        in_specs=[vmem, anywhere],
        out_specs=(anywhere, vmem),
        scratch_shapes=[
            pltpu.VMEM((planes, rows, 2 * count, width), jnp.bfloat16),
            pltpu.VMEM((planes, halves, MODES, rows, LANES), jnp.float32),
            pltpu.SemaphoreType.DMA((planes, parts)),
            pltpu.SemaphoreType.DMA((planes, halves, parts)),
        ],
        compiler_params=pltpu.CompilerParams(vmem_limit_bytes=60 * 1024 * 1024),
    )(gram, split)
    return (modes, basis)


def solution(mesh):
    return jax.shard_map(
        functools.partial(local, mesh.shape["gz"], mesh.shape["gy"]),
        mesh=mesh,
        in_specs=(P(None, "gz", "gy", None), P(), P("gz")),
        out_specs=(P(None, "gz", "gy", None), P()),
        check_vma=False,
    )
```

time: 293 us -> 182 us (0.62)
  Pallas kernels: 0 us -> 178 us
  waiting for transfers between devices: 133 us -> 0 us
  matrix products: 53.6 us -> 0 us
  other arithmetic: 49.7 us -> 0 us
  blocking collectives: 39.7 us -> 0 us
  starting transfers between devices: 7.08 us -> 0 us
  local copies, waits for them, and re-layouts: 8.63 us -> 2.75 us
    pallas_call x0 -> x2, Pallas kernels: none -> 178 us  [the longest x1 159 us: local(): pl.pallas_call(functools.partial(gram_kernel, gz_count, gy_count, total),...]
    ppermute x2 -> x0, waiting for transfers between devices: 133 us -> none  [the longest x1 131 us: padded_2(): lax.ppermute(lax.slice_in_dim(block, block.shape[dim] - width, None, axis...]
    dot_general x15 -> x0, matrix products: 52.4 us -> none  [the longest x1 32.1 us: local(): jnp.dot(weighted, flat.T, precision=lax.Precision.HIGHEST) / total]
    psum x1 -> x0, blocking collectives: 39.7 us -> none  [local(): gram = lax.psum(partial_value, ('gz', 'gy'))]
    mul x2 -> x0, other arithmetic: 25.5 us -> none  [the longest x1 13.5 us: local(): weighted = (filtered * plane_weight[None, :, None, None]).reshape(count, -1)]
    another operation x30 -> x0, other arithmetic: 24.1 us -> none  [the longest x18 12.9 us: local(): jnp.linalg.cholesky(jnp.dot(image.T, image, precision=lax.Precision.HIGHE...]
    ppermute x2 -> x0, starting transfers between devices: 7.08 us -> none  [the longest x1 4.06 us: padded_2(): lax.ppermute(lax.slice_in_dim(block, 0, width, axis=dim), axis, backward)]
    unnamed x7 -> x0, local copies, waits for them, and re-layouts: 4.45 us -> none
  transfers between devices with their start and end apart: 2 -> 0, of which waited for: 2 -> 0; matrix products, arithmetic and copies ran while one was open for 0% -> 0% of each run, Pallas kernels for 0% -> 0%
where the time goes in v1:
time: 182 us
  Pallas kernels  178 us (98%)
  local copies, waits for them, and re-layouts  2.75 us (2%)
    pallas_call x1, Pallas kernels, local(): pl.pallas_call(functools.partial(gram_kernel, gz_count, gy_count, total),...  159 us
    pallas_call x1, Pallas kernels, local(): pl.pallas_call(modes_kernel, name='basis_and_modes', out_shape=(jax.Shape...  19.5 us

profile of v1, /device:TPU:0, one launch (start us, length us, event | category | flops | bytes accessed | tf_op | source)
XLA Modules:
  0.0 181.6 jit_solution(193021502765801468)
XLA Ops:
  0.6 1.3 copy.5.energy_ref
  2.0 158.7 %exchange_and_gram.1 = (bf16[4,64,96,256]{3,2,1,0:T(8,128)(2,1)}, f32[48,48]{1,0:T(8,128)}) custom-call(f32[48,4,64,256]{3,2,1,0:T(8,128)} %snap_ref.1, f32[48,1]{1,0:T(8,128)} %copy.5.energy_ref, f32[4]{0:T(128)} %weight_ref.1), custom_call_target="tpu_custom_call" | custom-call | tf_op jit(solution)/shard_map/exchange_and_gram/pallas_call | solution.py:255
  160.7 19.5 %basis_and_modes.1 = (f32[16,4,64,256]{3,2,1,0:T(8,128)}, f32[48,16]{1,0:T(8,128)}) custom-call(f32[48,48]{1,0:T(8,128)} %get-tuple-element.4.gram_ref, bf16[4,64,96,256]{3,2,1,0:T(8,128)(2,1)} %get-tuple-element.5.split_ref), custom_call_target="tpu_custom_call" | custom-call | tf_op jit(solution)/shard_map/basis_and_modes/pallas_call | solution.py:282
  180.2 1.4 copy.6

commit v2 on v1

--- a/solution.py
+++ b/solution.py
@@ -16,18 +16,18 @@
 NT = (((1,), (1,)), ((), ()))
 
 
-def butterfly(index, bit):
-    return index + bit - 2 * bit * lax.rem(lax.div(index, bit), 2)
-
-
-def bits_of(count):
-    return [1 << k for k in range(count.bit_length() - 1)]
+def near_size(count):
+    size = 1
+    while size * size < count:
+        size *= 2
+    return size if count % size == 0 else 1
 
 
 def gram_kernel(
     gz_count, gy_count, total,
     snap_ref, energy_ref, weight_ref, split_ref, gram_ref,
-    own, halo, split, sums, arrived, own_sem, halo_send, halo_recv, split_sem, sum_send, sum_recv,
+    own, halo, split, near_sums, far_sums,
+    own_sem, halo_send, halo_recv, split_sem, near_send, near_recv, far_send, far_recv,
 ):
     count, planes, rows, width = snap_ref.shape
     chunks = rows // CHUNK
@@ -47,8 +47,18 @@
     for load in loads:
         load.start()
 
-    partners = [{"gy": butterfly(core, bit)} for bit in bits_of(gy_count)]
-    partners += [{"gz": butterfly(me, bit)} for bit in bits_of(gz_count)]
+    near = near_size(gz_count)
+    far = gz_count // near
+    inner = lax.rem(me, near)
+    outer = lax.div(me, near)
+    near_mine = inner * gy_count + core
+    near_peers = []
+    for k in range(1, near * gy_count):
+        peer = lax.rem(near_mine + k, near * gy_count)
+        place = outer * near + lax.div(peer, gy_count)
+        near_peers.append({"gz": place, "gy": lax.rem(peer, gy_count)})
+    far_peers = [{"gz": lax.rem(outer + k, far) * near + inner} for k in range(1, far)]
+    partners = near_peers + far_peers
     barrier = pltpu.get_barrier_semaphore()
     greeted = [{"gz": left}, {"gz": right}] + partners
     for device in greeted:
@@ -78,7 +88,10 @@
     for load in loads:
         load.wait()
 
-    energy = jnp.broadcast_to(energy_ref[...], (count, LANES))
+    column = lax.broadcasted_iota(jnp.int32, (count, count), 0)
+    lane = lax.broadcasted_iota(jnp.int32, (count, count), 1)
+    spread = jnp.where(column == lane, jnp.broadcast_to(energy_ref[...], (count, count)), 0.0)
+    energy = jnp.broadcast_to(jnp.sum(spread, axis=1, keepdims=True), (count, LANES))
 
     def flat(ref):
         return [ref.at[h].reshape(count * rows, LANES) for h in range(halves)]
@@ -128,19 +141,27 @@
     first, last = lax.fori_loop(0, chunks, edge, (zero, zero))
     gram = (gram + weight_ref[0] * first + weight_ref[planes - 1] * last) / total
 
-    for step, partner in enumerate(partners):
-        sums[step] = gram
-        copy = pltpu.make_async_remote_copy(
-            src_ref=sums.at[step],
-            dst_ref=arrived.at[step],
-            send_sem=sum_send.at[step],
-            recv_sem=sum_recv.at[step],
-            device_id=partner,
-            device_id_type=MESH,
-        )
-        copy.start()
-        copy.wait()
-        gram = gram + arrived[step]
+    def share(value, slots, mine, peers, send_sem, recv_sem):
+        slots[mine] = value
+        copies = [
+            pltpu.make_async_remote_copy(
+                src_ref=slots.at[mine],
+                dst_ref=slots.at[mine],
+                send_sem=send_sem.at[k],
+                recv_sem=recv_sem.at[k],
+                device_id=peer,
+                device_id_type=MESH,
+            )
+            for k, peer in enumerate(peers)
+        ]
+        for copy in copies:
+            copy.start()
+        for copy in copies:
+            copy.wait()
+        return sum(slots[k] for k in range(1, slots.shape[0])) + slots[0]
+
+    gram = share(gram, near_sums, near_mine, near_peers, near_send, near_recv)
+    gram = share(gram, far_sums, outer, far_peers, far_send, far_recv)
     gram_ref[...] = gram
 
     def drain(chunk, carry):
@@ -178,37 +199,39 @@
             load(z, p).start()
 
     gram = gram_ref[...]
-    row = lax.broadcasted_iota(jnp.int32, (MODES, 1), 0)
-    diagonal = (
-        lax.broadcasted_iota(jnp.int32, (MODES, MODES), 0)
-        == lax.broadcasted_iota(jnp.int32, (MODES, MODES), 1)
-    )
-
+    row = lax.broadcasted_iota(jnp.int32, (MODES, count), 0)
     def iterate(step, basis):
         image = jnp.dot(basis, gram, precision=HIGHEST, preferred_element_type=jnp.float32)
         square = lax.dot_general(
             image, image, NT, precision=HIGHEST, preferred_element_type=jnp.float32
         )
-        for j in range(MODES - 1):
-            inverse = 1.0 / square[j : j + 1, j : j + 1]
-            ratio = jnp.where(row > j, square[:, j : j + 1] * inverse, 0.0)
-            image = image - ratio * image[j : j + 1, :]
-            square = square - ratio * square[j : j + 1, :]
-        pivots = jnp.sum(jnp.where(diagonal, square, 0.0), axis=1, keepdims=True)
-        return image / jnp.sqrt(pivots)
+        columns = [
+            jnp.broadcast_to(square[:, j : j + 1], (MODES, count)) for j in range(MODES)
+        ]
+        scale = jnp.zeros((MODES, count), jnp.float32)
+        for j in range(MODES):
+            pivot = columns[j][j : j + 1, :]
+            scale = jnp.where(row == j, pivot, scale)
+            if j < MODES - 1:
+                ratio = jnp.where(row > j, columns[j] * (1.0 / pivot), 0.0)
+                for k in range(j + 1, MODES):
+                    columns[k] = columns[k] - ratio * columns[k][j : j + 1, :]
+                image = image - ratio * image[j : j + 1, :]
+        return image / jnp.sqrt(scale)
 
     start = (
         lax.broadcasted_iota(jnp.int32, (MODES, count), 0)
         == lax.broadcasted_iota(jnp.int32, (MODES, count), 1)
     ).astype(jnp.float32)
     basis = lax.fori_loop(0, ITERS, iterate, start)
-    basis_ref[...] = basis.T
+    basis_ref[...] = basis
     projected = jnp.dot(basis, gram, precision=HIGHEST, preferred_element_type=jnp.float32)
     norms = jnp.sum(basis * projected, axis=1, keepdims=True)
     scaled = basis / jnp.sqrt(norms)
-    high = scaled.astype(jnp.bfloat16)
-    low = (scaled - high.astype(jnp.float32)).astype(jnp.bfloat16)
-    both = jnp.concatenate([high, low], axis=0)
+    high = scaled.astype(jnp.bfloat16).astype(jnp.float32)
+    top = jnp.concatenate([high, high], axis=1)
+    bottom = jnp.concatenate([scaled - high, jnp.zeros_like(high)], axis=1)
+    both = jnp.concatenate([top, bottom], axis=0).astype(jnp.bfloat16)
 
     for z in range(planes):
         flat = [staged.at[z, h].reshape(MODES * rows, LANES) for h in range(halves)]
@@ -216,23 +239,14 @@
         def do_part(p, carry):
             load(z, p).wait()
 
-            def group(g, carry):
-                for r in range(8):
-                    y = p * part + g * 8 + r
-                    first = jnp.dot(
-                        both, split[z, y, :count], preferred_element_type=jnp.float32
-                    )
-                    second = jnp.dot(
-                        high, split[z, y, count:], preferred_element_type=jnp.float32
-                    )
-                    raw = first[:MODES] + (first[MODES:] + second)
-                    for h in range(halves):
-                        flat[h][pl.ds(y, MODES, stride=rows), :] = raw[
-                            :, h * LANES : (h + 1) * LANES
-                        ]
-                return carry
-
-            lax.fori_loop(0, part // 8, group, 0)
+            for r in range(part):
+                y = p * part + r
+                pair = jnp.dot(both, split[z, y], preferred_element_type=jnp.float32)
+                raw = pair[:MODES] + pair[MODES:]
+                for h in range(halves):
+                    flat[h][pl.ds(y, MODES, stride=rows), :] = raw[
+                        :, h * LANES : (h + 1) * LANES
+                    ]
             for h in range(halves):
                 store(z, p, h).start()
             return carry
@@ -249,7 +263,9 @@
     total = planes * gz_count * rows * gy_count * width
     chunks = rows // CHUNK
     halves = width // LANES
-    steps = len(bits_of(gz_count)) + len(bits_of(gy_count))
+    near = near_size(gz_count)
+    near_total = near * gy_count
+    far = gz_count // near
     anywhere = pl.BlockSpec(memory_space=pl.ANY)
     vmem = pl.BlockSpec(memory_space=pltpu.VMEM)
     split, gram = pl.pallas_call(
@@ -265,26 +281,28 @@
             pltpu.VMEM((planes, halves, count, rows, LANES), jnp.float32),
             pltpu.VMEM((2, halves, count, rows, LANES), jnp.float32),
             pltpu.VMEM((planes, rows, 2 * count, width), jnp.bfloat16),
-            pltpu.VMEM((steps, count, count), jnp.float32),
-            pltpu.VMEM((steps, count, count), jnp.float32),
+            pltpu.VMEM((near_total, count, count), jnp.float32),
+            pltpu.VMEM((far, count, count), jnp.float32),
             pltpu.SemaphoreType.DMA((planes, halves)),
             pltpu.SemaphoreType.DMA((2, halves, chunks)),
             pltpu.SemaphoreType.DMA((2, halves, chunks)),
             pltpu.SemaphoreType.DMA((planes, chunks)),
-            pltpu.SemaphoreType.DMA((steps,)),
-            pltpu.SemaphoreType.DMA((steps,)),
+            pltpu.SemaphoreType.DMA((near_total,)),
+            pltpu.SemaphoreType.DMA((near_total,)),
+            pltpu.SemaphoreType.DMA((far,)),
+            pltpu.SemaphoreType.DMA((far,)),
         ],
         compiler_params=pltpu.CompilerParams(
             collective_id=0, has_side_effects=True, vmem_limit_bytes=60 * 1024 * 1024
         ),
-    )(snapshots, energies[:, None], plane_weight)
-    parts = 4
+    )(snapshots, energies[None], plane_weight)
+    parts = 2
     modes, basis = pl.pallas_call(
         modes_kernel,
         name="basis_and_modes",
         out_shape=(
             jax.ShapeDtypeStruct((MODES, planes, rows, width), jnp.float32),
-            jax.ShapeDtypeStruct((count, MODES), jnp.float32),
+            jax.ShapeDtypeStruct((MODES, count), jnp.float32),
         ),
         in_specs=[vmem, anywhere],
         out_specs=(anywhere, vmem),
@@ -296,7 +314,7 @@
         ],
         compiler_params=pltpu.CompilerParams(vmem_limit_bytes=60 * 1024 * 1024),
     )(gram, split)
-    return (modes, basis)
+    return (modes, basis.T)
 
 
 def solution(mesh):

time: 182 us -> 167 us (0.918)
  Pallas kernels: 178 us -> 166 us
  local copies, waits for them, and re-layouts: 2.75 us -> 0 us
    pallas_call x1, Pallas kernels: 19.5 us -> 10.6 us  [local(): pl.pallas_call(modes_kernel, name='basis_and_modes', out_shape=(jax.Shape...]
    pallas_call x1, Pallas kernels: 159 us -> 155 us  [local(): pl.pallas_call(functools.partial(gram_kernel, gz_count, gy_count, total),...]
where the time goes in v2:
time: 167 us
  Pallas kernels  166 us (99%)
    pallas_call x1, Pallas kernels, local(): pl.pallas_call(functools.partial(gram_kernel, gz_count, gy_count, total),...  155 us
    pallas_call x1, Pallas kernels, local(): pl.pallas_call(modes_kernel, name='basis_and_modes', out_shape=(jax.Shape...  10.6 us

profile of v2, /device:TPU:0, one launch (start us, length us, event | category | flops | bytes accessed | tf_op | source)
XLA Modules:
  0.0 166.6 jit_solution(579425838113982474)
XLA Ops:
  0.6 155.4 %exchange_and_gram.1 = (bf16[4,64,96,256]{3,2,1,0:T(8,128)(2,1)}, f32[48,48]{1,0:T(8,128)}) custom-call(f32[48,4,64,256]{3,2,1,0:T(8,128)} %snap_ref.1, f32[1,48]{1,0:T(1,128)} %bitcast.2, f32[4]{0:T(128)} %weight_ref.1), custom_call_target="tpu_custom_call" | custom-call | tf_op jit(solution)/shard_map/exchange_and_gram/pallas_call | solution.py:271
  156.0 10.6 %basis_and_modes.1 = (f32[16,4,64,256]{3,2,1,0:T(8,128)}, f32[16,48]{1,0:T(8,128)}) custom-call(f32[48,48]{1,0:T(8,128)} %get-tuple-element.6.gram_ref, bf16[4,64,96,256]{3,2,1,0:T(8,128)(2,1)} %get-tuple-element.7.split_ref), custom_call_target="tpu_custom_call" | custom-call | tf_op jit(solution)/shard_map/basis_and_modes/pallas_call | solution.py:300

commit v3 on v2

--- a/solution.py
+++ b/solution.py
@@ -69,19 +69,19 @@
         span = pl.ds(pl.multiple_of(chunk * CHUNK, CHUNK), CHUNK)
         return pltpu.make_async_remote_copy(
             src_ref=snap_ref.at[
-                :, planes - 1 if side == 0 else 0, span, pl.ds(h * LANES, LANES)
+                :, (1 - side) * (planes - 1), span, pl.ds(h * LANES, LANES)
             ],
             dst_ref=halo.at[side, h, :, span],
             send_sem=halo_send.at[side, h, chunk],
             recv_sem=halo_recv.at[side, h, chunk],
-            device_id={"gz": right if side == 0 else left},
+            device_id={"gz": lax.rem(me + 1 - 2 * side + gz_count, gz_count)},
             device_id_type=MESH,
         )
 
     def send(chunk, carry):
         for h in range(halves):
-            halo_copy(0, chunk, h).start()
-            halo_copy(1, chunk, h).start()
+            halo_copy(1 - lax.rem(me, 2), chunk, h).start()
+            halo_copy(lax.rem(me, 2), chunk, h).start()
         return carry
 
     lax.fori_loop(0, chunks, send, 0)
@@ -104,39 +104,46 @@
             split.at[z, span], split_ref.at[z, span], split_sem.at[z, chunk]
         )
 
-    def add_rows(z, chunk, acc):
+    def add_rows(z, chunk, acc, begin=0, end=halves):
         below, middle, above = stack[z : z + 3]
         for r in range(CHUNK):
             y = chunk * CHUNK + r
             line = pl.ds(y, count, stride=rows)
             pieces = [
                 energy * (0.25 * (b[line, :] + a[line, :]) + 0.5 * m[line, :])
-                for b, m, a in zip(below, middle, above)
+                for b, m, a in zip(below[begin:end], middle[begin:end], above[begin:end])
             ]
             value = jnp.concatenate(pieces, axis=1)
             high = value.astype(jnp.bfloat16)
             low = (value - high.astype(jnp.float32)).astype(jnp.bfloat16)
             both = jnp.concatenate([high, low], axis=0)
-            split[z, y] = both
+            split[z, y, :, begin * LANES : end * LANES] = both
             first = lax.dot_general(both, high, NT, preferred_element_type=jnp.float32)
             second = lax.dot_general(high, low, NT, preferred_element_type=jnp.float32)
             acc = acc + (first[:count] + (first[count:] + second))
+        return acc
+
+    def add_inner(z, chunk, acc):
+        acc = add_rows(z, chunk, acc)
         split_copy(z, chunk).start()
         return acc
 
     zero = jnp.zeros((count, count), jnp.float32)
     gram = zero
     for z in range(1, planes - 1):
-        acc = lax.fori_loop(0, chunks, functools.partial(add_rows, z), zero)
+        acc = lax.fori_loop(0, chunks, functools.partial(add_inner, z), zero)
         gram = gram + weight_ref[z] * acc
 
     def edge(chunk, carry):
+        first, last = carry
         for h in range(halves):
             halo_copy(0, chunk, h).wait_recv()
-        first = add_rows(0, chunk, carry[0])
-        for h in range(halves):
+            first = add_rows(0, chunk, first, h, h + 1)
             halo_copy(1, chunk, h).wait_recv()
-        return first, add_rows(planes - 1, chunk, carry[1])
+            last = add_rows(planes - 1, chunk, last, h, h + 1)
+        split_copy(0, chunk).start()
+        split_copy(planes - 1, chunk).start()
+        return first, last
 
     first, last = lax.fori_loop(0, chunks, edge, (zero, zero))
     gram = (gram + weight_ref[0] * first + weight_ref[planes - 1] * last) / total
@@ -160,9 +167,24 @@
             copy.wait()
         return sum(slots[k] for k in range(1, slots.shape[0])) + slots[0]
 
-    gram = share(gram, near_sums, near_mine, near_peers, near_send, near_recv)
-    gram = share(gram, far_sums, outer, far_peers, far_send, far_recv)
-    gram_ref[...] = gram
+    third = count // 3
+    spare = near_sums.shape[2] - 2 * count
+    packed = jnp.concatenate(
+        [gram[k * third : (k + 1) * third, k * third :] for k in range(3)]
+        + [jnp.zeros((third, spare), jnp.float32)],
+        axis=1,
+    )
+    packed = share(packed, near_sums, near_mine, near_peers, near_send, near_recv)
+    packed = share(packed, far_sums, outer, far_peers, far_send, far_recv)
+    bands = [
+        packed[:, :count],
+        jnp.concatenate([zero[:third, :third], packed[:, count : 2 * count - third]], axis=1),
+        jnp.concatenate(
+            [zero[:third, : 2 * third], packed[:, 2 * count - third : 2 * count]], axis=1
+        ),
+    ]
+    upper = jnp.concatenate(bands, axis=0)
+    gram_ref[...] = jnp.where(column <= lane, upper, upper.T)
 
     def drain(chunk, carry):
         for h in range(halves):
@@ -281,8 +303,8 @@
             pltpu.VMEM((planes, halves, count, rows, LANES), jnp.float32),
             pltpu.VMEM((2, halves, count, rows, LANES), jnp.float32),
             pltpu.VMEM((planes, rows, 2 * count, width), jnp.bfloat16),
-            pltpu.VMEM((near_total, count, count), jnp.float32),
-            pltpu.VMEM((far, count, count), jnp.float32),
+            pltpu.VMEM((near_total, count // 3, LANES), jnp.float32),
+            pltpu.VMEM((far, count // 3, LANES), jnp.float32),
             pltpu.SemaphoreType.DMA((planes, halves)),
             pltpu.SemaphoreType.DMA((2, halves, chunks)),
             pltpu.SemaphoreType.DMA((2, halves, chunks)),

time: 167 us -> 165 us (0.988)
  Pallas kernels: 166 us -> 164 us
    pallas_call x1, Pallas kernels: 155 us -> 154 us  [local(): pl.pallas_call(functools.partial(gram_kernel, gz_count, gy_count, total),...]
where the time goes in v3:
time: 165 us
  Pallas kernels  164 us (99%)
    pallas_call x1, Pallas kernels, local(): pl.pallas_call(functools.partial(gram_kernel, gz_count, gy_count, total),...  154 us
    pallas_call x1, Pallas kernels, local(): pl.pallas_call(modes_kernel, name='basis_and_modes', out_shape=(jax.Shape...  10.6 us

profile of v3, /device:TPU:0, one launch (start us, length us, event | category | flops | bytes accessed | tf_op | source)
XLA Modules:
  0.0 164.7 jit_solution(7628771515870498294)
XLA Ops:
  0.6 153.5 %exchange_and_gram.1 = (bf16[4,64,96,256]{3,2,1,0:T(8,128)(2,1)}, f32[48,48]{1,0:T(8,128)}) custom-call(f32[48,4,64,256]{3,2,1,0:T(8,128)} %snap_ref.1, f32[1,48]{1,0:T(1,128)} %bitcast.2, f32[4]{0:T(128)} %weight_ref.1), custom_call_target="tpu_custom_call" | custom-call | tf_op jit(solution)/shard_map/exchange_and_gram/pallas_call | solution.py:293
  154.1 10.6 %basis_and_modes.1 = (f32[16,4,64,256]{3,2,1,0:T(8,128)}, f32[16,48]{1,0:T(8,128)}) custom-call(f32[48,48]{1,0:T(8,128)} %get-tuple-element.6.gram_ref, bf16[4,64,96,256]{3,2,1,0:T(8,128)(2,1)} %get-tuple-element.7.split_ref), custom_call_target="tpu_custom_call" | custom-call | tf_op jit(solution)/shard_map/basis_and_modes/pallas_call | solution.py:322

commit v4 on v3

--- a/solution.py
+++ b/solution.py
@@ -78,13 +78,13 @@
             device_id_type=MESH,
         )
 
-    def send(chunk, carry):
+    def send(step, carry):
+        side = lax.rem(me + 1 + lax.div(step, chunks), 2)
         for h in range(halves):
-            halo_copy(1 - lax.rem(me, 2), chunk, h).start()
-            halo_copy(lax.rem(me, 2), chunk, h).start()
+            halo_copy(side, lax.rem(step, chunks), h).start()
         return carry
 
-    lax.fori_loop(0, chunks, send, 0)
+    lax.fori_loop(0, 2 * chunks, send, 0)
     for load in loads:
         load.wait()
 

time: 165 us -> 165 us (level)
  no operation moved by 1% of the time
where the time goes in v4:
time: 165 us
  Pallas kernels  164 us (99%)
    pallas_call x1, Pallas kernels, local(): pl.pallas_call(functools.partial(gram_kernel, gz_count, gy_count, total),...  154 us
    pallas_call x1, Pallas kernels, local(): pl.pallas_call(modes_kernel, name='basis_and_modes', out_shape=(jax.Shape...  10.6 us

profile of v4, /device:TPU:0, one launch (start us, length us, event | category | flops | bytes accessed | tf_op | source)
XLA Modules:
  0.0 164.7 jit_solution(7949858252525522802)
XLA Ops:
  0.6 153.5 %exchange_and_gram.1 = (bf16[4,64,96,256]{3,2,1,0:T(8,128)(2,1)}, f32[48,48]{1,0:T(8,128)}) custom-call(f32[48,4,64,256]{3,2,1,0:T(8,128)} %snap_ref.1, f32[1,48]{1,0:T(1,128)} %bitcast.2, f32[4]{0:T(128)} %weight_ref.1), custom_call_target="tpu_custom_call" | custom-call | tf_op jit(solution)/shard_map/exchange_and_gram/pallas_call | solution.py:293
  154.2 10.6 %basis_and_modes.1 = (f32[16,4,64,256]{3,2,1,0:T(8,128)}, f32[16,48]{1,0:T(8,128)}) custom-call(f32[48,48]{1,0:T(8,128)} %get-tuple-element.6.gram_ref, bf16[4,64,96,256]{3,2,1,0:T(8,128)(2,1)} %get-tuple-element.7.split_ref), custom_call_target="tpu_custom_call" | custom-call | tf_op jit(solution)/shard_map/basis_and_modes/pallas_call | solution.py:322
